TPU v7x, 256 devices: a whole 4x4x8 slice. The times are simulated.
256 devices in a mesh: grp: 32 (over x, z), sub: 8 (over y, core).
Axes of the slice: x: 4, y: 4, z: 8, core: 2. Of those that a mesh axis runs over, the one named last changes fastest.
Arguments:
- ham_columns: bfloat16 [768, 5, 128, 128], P(('grp', 'sub')), may hold values from -2.2 to 2.2, as said below
- bond_mask: int32 [768, 4], P(('grp', 'sub')), may hold values 0 or 1
- owned_counts: int32 [32, 8], replicated, may hold values from 1 to 3, as said below
- fermi_level: float32 [1], replicated, may hold values from -0.5 to 0.5
Outputs:
- density: bfloat16 [768, 9, 128, 128], P(('grp', 'sub'))
Inputs may be any that keep to these rules, and one draw needn't show every extreme that they name: `ham_columns`: block 0 of every stored block column is symmetric. `bond_mask`: bond lists of slots that hold no cluster are never read. `owned_counts`: along sub, the devices 2k and 2k + 1 of a group own 2 * 2 block columns together, so group g owns clusters g * 16 to (g + 1) * 16 - 1, handed to its devices in order along sub in consecutive runs; no device owns exactly 2; every row has a device that owns 3.
All inputs are finite; a program needn't handle non-finite values. No bound on the sum of `bond_mask` on one device may be relied on, other than what follows from the above.
Results may differ from a plain program's by a relative error of at most 0.0025.
Values may be sent and summed in bfloat16 or wider, within the bound.
No kernel may reach another device: no remote copies, remote signals or barrier semaphores. Data moves between devices by JAX's collectives and lax.ppermute only.
A program may use at most 64 MiB of HBM per device.

v0:
```python
import jax
import jax.numpy as jnp
from jax import lax
from jax.sharding import PartitionSpec as P

COLS_MEAN = 2
spectral_span = 4.0


def extended(array, sides, width):
    for axis, dim in sides:
        size, length = (lax.axis_size(axis), array.shape[dim])
        up = [(i, (i + 1) % size) for i in range(size)]
        down = [(j, i) for i, j in up]
        last = lax.slice_in_dim(array, length - width, length, axis=dim)
        leading = lax.slice_in_dim(array, 0, width, axis=dim)
        before = lax.ppermute(last, axis, up)
        after = lax.ppermute(leading, axis, down)
        array = jnp.concatenate([before, array, after], axis=dim)
    return array


def partner(value, axis, distance):
    mask = 2**distance
    pairs = [(source, source ^ mask) for source in range(lax.axis_size(axis))]
    return lax.ppermute(value, axis, pairs)


def build_tile(window_cols, window_bonds, chemical):
    reach_len = window_bonds.shape[1]
    window_len = window_cols.shape[0]
    block_width = window_cols.shape[2]
    identity = jnp.eye(block_width, dtype=jnp.float32)
    bond_values = window_bonds.astype(jnp.float32)
    living = []
    for member in range(window_len):
        if member == reach_len:
            living.append(jnp.ones((), jnp.float32))
        elif member > reach_len:
            living.append(bond_values[reach_len, member - reach_len - 1])
        else:
            living.append(bond_values[member, reach_len - member - 1])
    rows_list = []
    for row_blk in range(window_len):
        pieces = []
        for col_blk in range(window_len):
            distance = row_blk - col_blk
            weight = living[row_blk] * living[col_blk]
            if distance == 0:
                block_value = (
                    window_cols[row_blk, 0].astype(jnp.float32) - chemical * identity
                ) * weight
            elif 0 < distance <= reach_len:
                block_value = window_cols[col_blk, distance].astype(jnp.float32) * (
                    weight * bond_values[col_blk, distance - 1]
                )
            elif 0 < -distance <= reach_len:
                block_value = window_cols[row_blk, -distance].astype(jnp.float32).T * (
                    weight * bond_values[row_blk, -distance - 1]
                )
            else:
                block_value = jnp.zeros((block_width, block_width), jnp.float32)
            pieces.append(block_value)
        rows_list.append(jnp.concatenate(pieces, axis=1))
    return (jnp.concatenate(rows_list, axis=0) / spectral_span).astype(jnp.bfloat16)


def product(matrix, vector):
    return jnp.dot(matrix, vector.astype(jnp.bfloat16), preferred_element_type=jnp.float32)


def apply_rest(matrix, first_term):
    second = product(matrix, first_term)
    third_term = product(matrix, second)
    return 1.5 * first_term - 0.5 * third_term


def density_column(matrix, window_len, block_width):
    center = (window_len - 1) // 2
    first_term = matrix[:, center * block_width : (center + 1) * block_width].astype(jnp.float32)
    step_one = apply_rest(matrix, first_term)
    step_two = apply_rest(matrix, product(matrix, step_one))
    step_three = apply_rest(matrix, product(matrix, step_two))
    sign_column = 1.5 * step_one - 0.5 * step_three
    above = jnp.zeros((center * block_width, block_width), jnp.float32)
    selector = jnp.concatenate([above, jnp.eye(block_width, dtype=jnp.float32), above], axis=0)
    result = (0.5 * (selector - sign_column)).astype(jnp.bfloat16)
    return result.reshape(window_len, block_width, block_width)


def window_result(run_cols, run_bonds, first_row, chemical):
    window_len = 2 * run_bonds.shape[1] + 1
    block_width = run_cols.shape[2]
    window_cols = lax.dynamic_slice_in_dim(run_cols, first_row, window_len, 0)
    window_bonds = lax.dynamic_slice_in_dim(run_bonds, first_row, window_len, 0)
    matrix = build_tile(window_cols, window_bonds, chemical)
    return density_column(matrix, window_len, block_width)


def body(ham_columns, bond_mask, owned_counts, fermi_level):
    reach_len = bond_mask.shape[1]
    slots_here = ham_columns.shape[0]
    group_size = lax.axis_size("sub")
    chemical = fermi_level[0]
    counts_flat = owned_counts.reshape(-1)
    group_index = lax.axis_index("grp")
    member_index = lax.axis_index("sub")
    device_index = group_index * group_size + member_index
    my_count = counts_flat[device_index]
    slot_range = jnp.arange(slots_here, dtype=jnp.int32)
    in_use = slot_range < my_count
    gathered_cols, gathered_bonds = (
        lax.all_gather(ham_columns, "sub", axis=0, tiled=True),
        lax.all_gather(bond_mask, "sub", axis=0, tiled=True),
    )
    group_counts = lax.dynamic_index_in_dim(owned_counts, group_index, 0, keepdims=False)
    group_ends = jnp.cumsum(group_counts)
    group_starts = group_ends - group_counts
    group_cols = COLS_MEAN * group_size
    positions = jnp.arange(group_cols, dtype=jnp.int32)
    owner_index = jnp.sum((group_ends[None, :] <= positions[:, None]).astype(jnp.int32), axis=1)
    gather_index = owner_index * slots_here + positions - group_starts[owner_index]
    local_cols = jnp.take(gathered_cols, gather_index, axis=0)
    local_bonds = jnp.take(gathered_bonds, gather_index, axis=0)
    edge_cols, edge_bonds = (
        extended(local_cols, (("grp", 0),), reach_len),
        extended(local_bonds, (("grp", 0),), reach_len),
    )
    first_rows = member_index * COLS_MEAN + jnp.arange(COLS_MEAN, dtype=jnp.int32)
    results = lax.map(
        lambda first_row: window_result(edge_cols, edge_bonds, first_row, chemical), first_rows
    )
    partner_results = partner(results, "sub", 0)
    is_odd = member_index % 2
    lower_first = jnp.concatenate([results, partner_results], axis=0)
    upper_first = jnp.concatenate([partner_results, results], axis=0)
    pair_results = jnp.where(is_odd == 0, lower_first, upper_first)
    pair_start = (member_index - is_odd) * COLS_MEAN
    wanted = jnp.minimum(group_starts[member_index] - pair_start + slot_range, 2 * COLS_MEAN - 1)
    picked = jnp.take(pair_results, wanted, axis=0)
    return jnp.where(in_use[:, None, None, None], picked, jnp.zeros_like(picked))


def solution(mesh):
    placed = (P(("grp", "sub"), None, None, None), P(("grp", "sub"), None), P(), P())
    return jax.shard_map(
        body,
        mesh=mesh,
        in_specs=placed,
        out_specs=P(("grp", "sub"), None, None, None),
        check_vma=False,
    )
```

profile of v0, /device:TPU:1, one launch (start us, length us, event | category | flops | bytes accessed | tf_op | source)
XLA Modules:
  0.0 367.3 jit_solution(13713588425739931471)
XLA Ops:
  8.3 14.4 %all-gather = s32[8,3,4]{2,1,0:T(4,128)S(1)} all-gather(s32[1,3,4]{2,1,0:T(4,128)} %bitcast.405), channel_id=1, replica_groups=mesh['grp'=32,'sub'=8] {'sub'}, dimensions={0}, use_global_device_ids=true | all-gather | bytes 432 | tf_op jit(solution)/shard_map/all_gather | solution.py:114
  24.2 22.8 %all-gather.3.cloned.1.call-done = bf16[24,5,128,128]{3,2,1,0:T(8,128)(2,1)} async-done(((bf16[3,5,128,128]{3,2,1,0:T(8,128)(2,1)}), bf16[24,5,128,128]{3,2,1,0:T(8,128)(2,1)}) %all-gather.3.cloned.1.call-update) | async-done | bytes 3932176 | tf_op jit(solution)/shard_map/all_gather | solution.py:113
  46.9 4.5 %gather_fusion.1 = bf16[16,5,128,128]{3,2,1,0:T(8,128)(2,1)} fusion(bf16[24,5,128,128]{3,2,1,0:T(8,128)(2,1)} %all-gather.3.cloned.1.call-done, s32[1024]{0:T(1024)S(1)} %pad_clamp_fusion.1), kind=kCustom, calls=%fused_computation.1 | custom fusion | bytes 5242944 | tf_op jit(solution)/shard_map/jit(_take)/gather | solution.py:123
  51.4 2.1 broadcast_select_fusion
  54.5 5.2 %collective-permute-start.1 = (bf16[4,5,128,128]{3,2,1,0:T(8,128)(2,1)}, bf16[4,5,128,128]{3,2,1,0:T(8,128)(2,1)}, u32[]{:S(2)}, u32[]{:S(2)}) collective-permute-start(bf16[4,5,128,128]{3,2,1,0:T(8,128)(2,1)} %get-tuple-element.119), channel_id=1, source_target_pairs={{8,0},{16,8},{24,16},{32,24},{40,32},{48,40},{56,48},{64,56},{72,6... | collective-permute-start | bytes 1966088 | tf_op jit(solution)/shard_map/ppermute | solution.py:18
  59.7 4.8 %collective-permute-start.3 = (s32[4,4]{1,0:T(4,128)S(1)}, s32[4,4]{1,0:T(4,128)S(1)}, u32[]{:S(2)}, u32[]{:S(2)}) collective-permute-start(s32[4,4]{1,0:T(4,128)S(1)} %get-tuple-element.121), channel_id=1, source_target_pairs={{8,0},{16,8},{24,16},{32,24},{40,32},{48,40},{56,48},{64,56},{72,6... | collective-permute-start | bytes 200 | tf_op jit(solution)/shard_map/ppermute | solution.py:18
  64.6 9.2 %collective-permute-done.3 = s32[4,4]{1,0:T(4,128)S(1)} collective-permute-done((s32[4,4]{1,0:T(4,128)S(1)}, s32[4,4]{1,0:T(4,128)S(1)}, u32[]{:S(2)}, u32[]{:S(2)}) %collective-permute-start.3) | collective-permute-done | bytes 96 | tf_op jit(solution)/shard_map/ppermute | solution.py:18
  73.8 5.0 %collective-permute-done.2 = s32[4,4]{1,0:T(4,128)S(1)} collective-permute-done((s32[4,4]{1,0:T(4,128)S(1)}, s32[4,4]{1,0:T(4,128)S(1)}, u32[]{:S(2)}, u32[]{:S(2)}) %collective-permute-start.2) | collective-permute-done | bytes 96 | tf_op jit(solution)/shard_map/ppermute | solution.py:17
  79.0 3.3 pad_maximum_fusion
  82.3 270.8 %while.10 = (s32[]{:T(128)}, bf16[2,9,128,128]{3,2,1,0:T(8,128)(2,1)}, s32[2]{0:T(128)S(1)}, bf16[24,5,128,128]{3,2,1,0:T(8,128)(2,1)}, f32[]{:T(128)}, /*index=...) while((s32[]{:T(128)}, ...), condition=%wide.region_3.4_spmd, body=%wide.region_2.3_spmd.sunk | while | flops 2726674432 | bytes 48746780 | solution.py:130
  86.9 2.1 constant_dynamic-update-slice_fusion.81
  112.2 2.1 fusion.119
  125.8 2.0 fusion.120
  164.4 2.1 fusion.122
  179.7 2.1 fusion.124
  189.5 2.1 fusion.126
  198.0 2.1 fusion.128
  200.0 2.9 multiply_convert_fusion.2
  203.6 3.3 fusion.130
  209.7 3.3 fusion.132
  213.0 3.9 %fusion.133 = bf16[1152,128]{1,0:T(8,128)(2,1)S(1)} fusion(bf16[1152,1152]{1,0:T(8,128)(2,1)S(1)} %multiply_convert_fusion.2, f32[512,128]{1,0:T(8,128)S(1)} %broadcast.398, f32[128,128]{1,0:T(8,128)} %fusion.129, f32[1152,128]{1,0:T(8,128)} %fusion.132, f32[1152,128]{1,0:T(8,128)} %fusion.130), kind=kOutput, calls=%fused_computation.16.clone.1 | convolution fusion | flops 681394176 | bytes 4456448 | tf_op jit(solution)/shard_map/while/body/eval_jaxpr/dot_general | solution.py:69
  222.3 2.1 constant_dynamic-update-slice_fusion.81
  247.7 2.1 fusion.119
  261.3 2.0 fusion.120
  299.8 2.1 fusion.122
  315.1 2.1 fusion.124
  324.9 2.1 fusion.126
  333.4 2.1 fusion.128
  335.5 2.9 multiply_convert_fusion.2
  339.0 3.3 fusion.130
  345.1 3.3 fusion.132
  348.4 3.9 %fusion.133 = bf16[1152,128]{1,0:T(8,128)(2,1)S(1)} fusion(bf16[1152,1152]{1,0:T(8,128)(2,1)S(1)} %multiply_convert_fusion.2, f32[512,128]{1,0:T(8,128)S(1)} %broadcast.398, f32[128,128]{1,0:T(8,128)} %fusion.129, f32[1152,128]{1,0:T(8,128)} %fusion.132, f32[1152,128]{1,0:T(8,128)} %fusion.130), kind=kOutput, calls=%fused_computation.16.clone.1 | convolution fusion | flops 681394176 | bytes 4456448 | tf_op jit(solution)/shard_map/while/body/eval_jaxpr/dot_general | solution.py:69
  (253 shorter events, 133.5 us)
Async XLA Ops:
  6.5 40.4 %all-gather.3.cloned.1.call-start = ((), (), s32[]{:S(2)}) async-start(), calls=%async_computation | async-start | bytes 4423680 | tf_op jit(solution)/shard_map/all_gather | solution.py:113
  54.5 24.5 %collective-permute-start.1 = (bf16[4,5,128,128]{3,2,1,0:T(8,128)(2,1)}, bf16[4,5,128,128]{3,2,1,0:T(8,128)(2,1)}, u32[]{:S(2)}, u32[]{:S(2)}) collective-permute-start(bf16[4,5,128,128]{3,2,1,0:T(8,128)(2,1)} %get-tuple-element.119), channel_id=1, source_target_pairs={{8,0},{16,8},{24,16},{32,24},{40,32},{48,40},{56,48},{64,56},{72,6... | collective-permute-start | bytes 1966088 | tf_op jit(solution)/shard_map/ppermute | solution.py:18
  59.6 19.4 %collective-permute-start = (bf16[4,5,128,128]{3,2,1,0:T(8,128)(2,1)S(1)}, bf16[4,5,128,128]{3,2,1,0:T(8,128)(2,1)}, u32[]{:S(2)}, u32[]{:S(2)}) collective-permute-start(bf16[4,5,128,128]{3,2,1,0:T(8,128)(2,1)S(1)} %get-tuple-element.118), channel_id=1, source_target_pairs={{0,8},{8,16},{16,24},{24,32},{32,40},{40,48},{48,56},{56,64},{64,7... | collective-permute-start | bytes 1966088 | tf_op jit(solution)/shard_map/ppermute | solution.py:17
  59.7 14.1 %collective-permute-start.3 = (s32[4,4]{1,0:T(4,128)S(1)}, s32[4,4]{1,0:T(4,128)S(1)}, u32[]{:S(2)}, u32[]{:S(2)}) collective-permute-start(s32[4,4]{1,0:T(4,128)S(1)} %get-tuple-element.121), channel_id=1, source_target_pairs={{8,0},{16,8},{24,16},{32,24},{40,32},{48,40},{56,48},{64,56},{72,6... | collective-permute-start | bytes 200 | tf_op jit(solution)/shard_map/ppermute | solution.py:18
  64.5 14.3 %collective-permute-start.2 = (s32[4,4]{1,0:T(4,128)S(1)}, s32[4,4]{1,0:T(4,128)S(1)}, u32[]{:S(2)}, u32[]{:S(2)}) collective-permute-start(s32[4,4]{1,0:T(4,128)S(1)} %get-tuple-element.120), channel_id=1, source_target_pairs={{0,8},{8,16},{16,24},{24,32},{32,40},{40,48},{48,56},{56,64},{64,7... | collective-permute-start | bytes 200 | tf_op jit(solution)/shard_map/ppermute | solution.py:17
  82.3 272.2 %copy-start = (s32[32,8]{0,1:T(8,128)S(1)}, s32[32,8]{0,1:T(8,128)}, u32[]{:S(2)}) copy-start(s32[32,8]{0,1:T(8,128)} %param.8) | copy-start | bytes 3076
  353.1 4.1 %collective-permute-start.4 = (bf16[2,9,128,128]{3,2,1,0:T(8,128)(2,1)}, bf16[2,9,128,128]{3,2,1,0:T(8,128)(2,1)S(1)}, u32[]{:S(2)}, u32[]{:S(2)}) collective-permute-start(bf16[2,9,128,128]{3,2,1,0:T(8,128)(2,1)} %get-tuple-element.37), channel_id=1, source_target_pairs={{0,1},{1,0},{2,3},{3,2},{4,5},{5,4},{6,7},{7,6},{8,9},{9,8},{10,11... | collective-permute-start | bytes 1769480 | tf_op jit(solution)/shard_map/ppermute | solution.py:26
Sparse Core Ops, SparseCore 0:
  9.2 37.7 all-gather.2
where the time goes:
time: 374 us; the launch traced here: 367 us
  other arithmetic  116 us (31%)
  loops' own time  92.8 us (25%)
  local copies, waits for them, and re-layouts  54.5 us (15%)
  waiting for transfers between devices  37.6 us (10%)
  matrix products  26.7 us (7%)
  blocking collectives  14.4 us (4%)
  between operations  14.1 us (4%)
  starting transfers between devices  11.4 us (3%)
    another operation x1, loops' own time, body(): lax.map(lambda first_row: window_result(edge_cols, edge_bonds, first_row,...  92.8 us
    while x84, other arithmetic  90.3 us
    while x72, local copies, waits for them, and re-layouts  33.7 us
    dot_general x10, matrix products, product(): jnp.dot(matrix, vector.astype(jnp.bfloat16), preferred_element_type=jnp.f...  26.7 us
    all_gather x1, waiting for transfers between devices, body(): lax.all_gather(ham_columns, 'sub', axis=0, tiled=True)  22.8 us
    all_gather x1, blocking collectives, body(): lax.all_gather(bond_mask, 'sub', axis=0, tiled=True)  14.4 us
    ppermute x2, starting transfers between devices, extended(): after = lax.ppermute(leading, axis, down)  9.97 us
    ppermute x2, waiting for transfers between devices, extended(): after = lax.ppermute(leading, axis, down)  9.16 us
  transfers between devices with their start and end apart: 6, of which 3 were waited for; matrix products, arithmetic and copies ran while one was open for 1% of the time, Pallas kernels for 0%

commit v1 on v0

--- a/solution.py
+++ b/solution.py
@@ -5,6 +5,11 @@
 
 COLS_MEAN = 2
 spectral_span = 4.0
+
+
+def gather_from_all(x, axis, dim):
+    copies = jnp.concatenate([x] * lax.axis_size(axis), axis=dim)
+    return lax.all_to_all(copies, axis, dim, dim, tiled=True)
 
 
 def extended(array, sides, width):
@@ -110,7 +115,7 @@
     slot_range = jnp.arange(slots_here, dtype=jnp.int32)
     in_use = slot_range < my_count
     gathered_cols, gathered_bonds = (
-        lax.all_gather(ham_columns, "sub", axis=0, tiled=True),
+        gather_from_all(ham_columns, "sub", 0),
         lax.all_gather(bond_mask, "sub", axis=0, tiled=True),
     )
     group_counts = lax.dynamic_index_in_dim(owned_counts, group_index, 0, keepdims=False)

time: 374 us -> 393 us (1.051)
  blocking collectives: 14.4 us -> 51 us
  waiting for transfers between devices: 37.6 us -> 14.3 us
  between operations: 14.1 us -> 0.75 us
  local copies, waits for them, and re-layouts: 54.5 us -> 66.6 us
  starting transfers between devices: 11.4 us -> 19.8 us
    all_gather x1, blocking collectives: 14.4 us -> 51 us  [body(): lax.all_gather(bond_mask, 'sub', axis=0, tiled=True)]
    all_gather x1 -> x0, waiting for transfers between devices: 22.8 us -> none  [body(): lax.all_gather(ham_columns, 'sub', axis=0, tiled=True)]
    unnamed x4 -> x15, local copies, waits for them, and re-layouts: 0.09 us -> 12.2 us
    all_to_all x0 -> x1, starting transfers between devices: none -> 7.6 us  [gather_from_all(): return lax.all_to_all(copies, axis, dim, dim, tiled=True)]
  transfers between devices with their start and end apart: 6 -> 6, of which waited for: 3 -> 2; matrix products, arithmetic and copies ran while one was open for 1% -> 1% of each run, Pallas kernels for 0% -> 0%
where the time goes in v1:
time: 393 us; the launch traced here: 386 us
  other arithmetic  116 us (30%)
  loops' own time  91.3 us (23%)
  local copies, waits for them, and re-layouts  66.6 us (17%)
  blocking collectives  51 us (13%)
  matrix products  26.7 us (7%)
  starting transfers between devices  19.8 us (5%)
  waiting for transfers between devices  14.3 us (4%)
    another operation x1, loops' own time, body(): lax.map(lambda first_row: window_result(edge_cols, edge_bonds, first_row,...  91.3 us
    while x84, other arithmetic  90.3 us
    all_gather x1, blocking collectives, body(): lax.all_gather(bond_mask, 'sub', axis=0, tiled=True)  51 us
    while x72, local copies, waits for them, and re-layouts  33.6 us
    dot_general x10, matrix products, product(): jnp.dot(matrix, vector.astype(jnp.bfloat16), preferred_element_type=jnp.f...  26.7 us
    unnamed x15, local copies, waits for them, and re-layouts  12.2 us
    ppermute x2, starting transfers between devices, extended(): after = lax.ppermute(leading, axis, down)  10.9 us
    ppermute x2, waiting for transfers between devices, extended(): after = lax.ppermute(leading, axis, down)  9.27 us
  transfers between devices with their start and end apart: 6, of which 2 were waited for; matrix products, arithmetic and copies ran while one was open for 1% of the time, Pallas kernels for 0%

profile of v1, /device:TPU:1, one launch (start us, length us, event | category | flops | bytes accessed | tf_op | source)
XLA Modules:
  0.0 386.2 jit_solution(9080683137967743074)
XLA Ops:
  12.9 7.6 %all-to-all-start = ((bf16[24,5,128,128]{3,2,1,0:T(8,128)(2,1)}), bf16[24,5,128,128]{3,2,1,0:T(8,128)(2,1)}, u32[]{:S(2)}, u32[]{:S(2)}) async-start(bf16[24,5,128,128]{3,2,1,0:T(8,128)(2,1)} %constant_dynamic-update-slice_fusion.42), calls=%async_computation | async-start | bytes 7864320 | tf_op jit(solution)/shard_map/all_to_all | solution.py:12
  20.9 51.0 %all-gather = s32[8,3,4]{2,1,0:T(4,128)S(1)} all-gather(s32[1,3,4]{2,1,0:T(4,128)S(1)} %bitcast.405), channel_id=1, replica_groups=mesh['grp'=32,'sub'=8] {'sub'}, dimensions={0}, use_global_device_ids=true | all-gather | bytes 432 | tf_op jit(solution)/shard_map/all_gather | solution.py:119
  73.3 4.5 %gather_fusion.1 = bf16[16,5,128,128]{3,2,1,0:T(8,128)(2,1)} fusion(bf16[24,5,128,128]{3,2,1,0:T(8,128)(2,1)} %all-to-all-done, s32[1024]{0:T(1024)S(1)} %pad_clamp_fusion.1), kind=kCustom, calls=%fused_computation.1 | custom fusion | bytes 5242944 | tf_op jit(solution)/shard_map/jit(_take)/gather | solution.py:128
  77.8 2.1 broadcast_select_fusion
  80.8 6.1 %collective-permute-start.1 = (bf16[4,5,128,128]{3,2,1,0:T(8,128)(2,1)}, bf16[4,5,128,128]{3,2,1,0:T(8,128)(2,1)}, u32[]{:S(2)}, u32[]{:S(2)}) collective-permute-start(bf16[4,5,128,128]{3,2,1,0:T(8,128)(2,1)} %get-tuple-element.119), channel_id=1, source_target_pairs={{8,0},{16,8},{24,16},{32,24},{40,32},{48,40},{56,48},{64,56},{72,6... | collective-permute-start | bytes 1966088 | tf_op jit(solution)/shard_map/ppermute | solution.py:23
  87.0 4.8 %collective-permute-start.3 = (s32[4,4]{1,0:T(4,128)S(1)}, s32[4,4]{1,0:T(4,128)S(1)}, u32[]{:S(2)}, u32[]{:S(2)}) collective-permute-start(s32[4,4]{1,0:T(4,128)S(1)} %get-tuple-element.121), channel_id=1, source_target_pairs={{8,0},{16,8},{24,16},{32,24},{40,32},{48,40},{56,48},{64,56},{72,6... | collective-permute-start | bytes 200 | tf_op jit(solution)/shard_map/ppermute | solution.py:23
  91.9 9.3 %collective-permute-done.3 = s32[4,4]{1,0:T(4,128)S(1)} collective-permute-done((s32[4,4]{1,0:T(4,128)S(1)}, s32[4,4]{1,0:T(4,128)S(1)}, u32[]{:S(2)}, u32[]{:S(2)}) %collective-permute-start.3) | collective-permute-done | bytes 96 | tf_op jit(solution)/shard_map/ppermute | solution.py:23
  101.3 5.0 %collective-permute-done.2 = s32[4,4]{1,0:T(4,128)S(1)} collective-permute-done((s32[4,4]{1,0:T(4,128)S(1)}, s32[4,4]{1,0:T(4,128)S(1)}, u32[]{:S(2)}, u32[]{:S(2)}) %collective-permute-start.2) | collective-permute-done | bytes 96 | tf_op jit(solution)/shard_map/ppermute | solution.py:22
  106.4 3.3 pad_maximum_fusion
  109.7 269.3 %while.10 = (s32[]{:T(128)}, bf16[2,9,128,128]{3,2,1,0:T(8,128)(2,1)}, s32[2]{0:T(128)S(1)}, bf16[24,5,128,128]{3,2,1,0:T(8,128)(2,1)}, f32[]{:T(128)}, /*index=...) while((s32[]{:T(128)}, ...), condition=%wide.region_3.4_spmd, body=%wide.region_2.3_spmd.sunk | while | flops 2726674432 | bytes 48746780 | solution.py:135
  114.1 2.1 constant_dynamic-update-slice_fusion.89
  139.5 2.1 fusion.119
  149.5 2.1 constant_dynamic-update-slice_fusion.98
  152.9 2.1 fusion.120
  206.3 2.0 fusion.124
  216.1 2.1 fusion.126
  224.6 2.1 fusion.128
  226.7 2.9 multiply_convert_fusion.2
  230.2 3.3 fusion.130
  236.3 3.3 fusion.132
  239.7 3.9 %fusion.133 = bf16[1152,128]{1,0:T(8,128)(2,1)S(1)} fusion(bf16[1152,1152]{1,0:T(8,128)(2,1)S(1)} %multiply_convert_fusion.2, f32[512,128]{1,0:T(8,128)S(1)} %broadcast.398, f32[128,128]{1,0:T(8,128)} %fusion.129, f32[1152,128]{1,0:T(8,128)} %fusion.132, f32[1152,128]{1,0:T(8,128)} %fusion.130), kind=kOutput, calls=%fused_computation.16.clone.1 | convolution fusion | flops 681394176 | bytes 4456448 | tf_op jit(solution)/shard_map/while/body/eval_jaxpr/dot_general | solution.py:74
  248.7 2.1 constant_dynamic-update-slice_fusion.89
  274.2 2.1 fusion.119
  284.1 2.1 constant_dynamic-update-slice_fusion.98
  287.6 2.1 fusion.120
  341.0 2.0 fusion.124
  350.8 2.1 fusion.126
  359.3 2.1 fusion.128
  361.3 2.9 multiply_convert_fusion.2
  364.9 3.3 fusion.130
  371.0 3.3 fusion.132
  374.3 3.9 %fusion.133 = bf16[1152,128]{1,0:T(8,128)(2,1)S(1)} fusion(bf16[1152,1152]{1,0:T(8,128)(2,1)S(1)} %multiply_convert_fusion.2, f32[512,128]{1,0:T(8,128)S(1)} %broadcast.398, f32[128,128]{1,0:T(8,128)} %fusion.129, f32[1152,128]{1,0:T(8,128)} %fusion.132, f32[1152,128]{1,0:T(8,128)} %fusion.130), kind=kOutput, calls=%fused_computation.16.clone.1 | convolution fusion | flops 681394176 | bytes 4456448 | tf_op jit(solution)/shard_map/while/body/eval_jaxpr/dot_general | solution.py:74
  (264 shorter events, 144.9 us)
Async XLA Ops:
  0.0 11.3 %copy-start = (bf16[3,5,128,128]{3,2,1,0:T(8,128)(2,1)S(1)}, bf16[3,5,128,128]{3,2,1,0:T(8,128)(2,1)}, u32[]{:S(2)}) copy-start(bf16[3,5,128,128]{3,2,1,0:T(8,128)(2,1)} %param.6) | copy-start | bytes 1474564
  9.4 11.2 %copy-start.1 = (s32[32,8]{0,1:T(8,128)S(1)}, s32[32,8]{0,1:T(8,128)}, u32[]{:S(2)}) copy-start(s32[32,8]{0,1:T(8,128)} %param.8) | copy-start | bytes 3076
  9.4 11.5 %copy-start.2 = (s32[3,4]{1,0:T(4,128)S(1)}, s32[3,4]{1,0:T(4,128)}, u32[]{:S(2)}) copy-start(s32[3,4]{1,0:T(4,128)} %param.7) | copy-start | bytes 148
  12.9 60.4 %all-to-all-start = ((bf16[24,5,128,128]{3,2,1,0:T(8,128)(2,1)}), bf16[24,5,128,128]{3,2,1,0:T(8,128)(2,1)}, u32[]{:S(2)}, u32[]{:S(2)}) async-start(bf16[24,5,128,128]{3,2,1,0:T(8,128)(2,1)} %constant_dynamic-update-slice_fusion.42), calls=%async_computation | async-start | bytes 7864320 | tf_op jit(solution)/shard_map/all_to_all | solution.py:12
  80.8 25.6 %collective-permute-start.1 = (bf16[4,5,128,128]{3,2,1,0:T(8,128)(2,1)}, bf16[4,5,128,128]{3,2,1,0:T(8,128)(2,1)}, u32[]{:S(2)}, u32[]{:S(2)}) collective-permute-start(bf16[4,5,128,128]{3,2,1,0:T(8,128)(2,1)} %get-tuple-element.119), channel_id=1, source_target_pairs={{8,0},{16,8},{24,16},{32,24},{40,32},{48,40},{56,48},{64,56},{72,6... | collective-permute-start | bytes 1966088 | tf_op jit(solution)/shard_map/ppermute | solution.py:23
  86.9 19.5 %collective-permute-start = (bf16[4,5,128,128]{3,2,1,0:T(8,128)(2,1)S(1)}, bf16[4,5,128,128]{3,2,1,0:T(8,128)(2,1)}, u32[]{:S(2)}, u32[]{:S(2)}) collective-permute-start(bf16[4,5,128,128]{3,2,1,0:T(8,128)(2,1)S(1)} %get-tuple-element.118), channel_id=1, source_target_pairs={{0,8},{8,16},{16,24},{24,32},{32,40},{40,48},{48,56},{56,64},{64,7... | collective-permute-start | bytes 1966088 | tf_op jit(solution)/shard_map/ppermute | solution.py:22
  87.0 14.2 %collective-permute-start.3 = (s32[4,4]{1,0:T(4,128)S(1)}, s32[4,4]{1,0:T(4,128)S(1)}, u32[]{:S(2)}, u32[]{:S(2)}) collective-permute-start(s32[4,4]{1,0:T(4,128)S(1)} %get-tuple-element.121), channel_id=1, source_target_pairs={{8,0},{16,8},{24,16},{32,24},{40,32},{48,40},{56,48},{64,56},{72,6... | collective-permute-start | bytes 200 | tf_op jit(solution)/shard_map/ppermute | solution.py:23
  91.8 14.4 %collective-permute-start.2 = (s32[4,4]{1,0:T(4,128)S(1)}, s32[4,4]{1,0:T(4,128)S(1)}, u32[]{:S(2)}, u32[]{:S(2)}) collective-permute-start(s32[4,4]{1,0:T(4,128)S(1)} %get-tuple-element.120), channel_id=1, source_target_pairs={{0,8},{8,16},{16,24},{24,32},{32,40},{40,48},{48,56},{56,64},{64,7... | collective-permute-start | bytes 200 | tf_op jit(solution)/shard_map/ppermute | solution.py:22
  379.0 4.0 %collective-permute-start.4 = (bf16[2,9,128,128]{3,2,1,0:T(8,128)(2,1)}, bf16[2,9,128,128]{3,2,1,0:T(8,128)(2,1)S(1)}, u32[]{:S(2)}, u32[]{:S(2)}) collective-permute-start(bf16[2,9,128,128]{3,2,1,0:T(8,128)(2,1)} %get-tuple-element.37), channel_id=1, source_target_pairs={{0,1},{1,0},{2,3},{3,2},{4,5},{5,4},{6,7},{7,6},{8,9},{9,8},{10,11... | collective-permute-start | bytes 1769480 | tf_op jit(solution)/shard_map/ppermute | solution.py:31
